TPU v7x, 32 devices: a whole 2x2x4 slice. The times are simulated.
32 devices in a mesh: seq: 8 (over z, x), dp: 4 (over y, core).
Axes of the slice: x: 2, y: 2, z: 4, core: 2. Of those that a mesh axis runs over, the one named last changes fastest.
Arguments:
- conv_input: bfloat16 [4, 2048, 2816], P('dp', 'seq'), may hold values from -6 to 6
- gate_input: bfloat16 [4, 2048, 2560], P('dp', 'seq'), may hold values from -6 to 6
- step_input: float32 [4, 40, 2048], P('dp', None, 'seq'), may hold values from -7.5 to 2048
- filter_taps: float32 [4, 2816], replicated, may hold values from -3 to 3
- filter_bias: float32 [2816], replicated, may hold values from -0.5 to 0.5
- step_bias: float32 [40], replicated, may hold values from -1 to 1
- decay_log: float32 [40], replicated, may hold values from -13 to 3
- skip_gain: float32 [40], replicated, may hold values from 0.5 to 1.5
- norm_weight: float32 [2560], replicated, may hold values from 0.5 to 1.5
- output_weight: bfloat16 [2560, 1280], P('dp'), may hold values from -0.125 to 0.125
- output_grad: bfloat16 [4, 2048, 1280], P('dp', 'seq'), may hold values from -6 to 6
Outputs:
- input_grad: bfloat16 [4, 2048, 2816], P('dp', 'seq')
- gate_grad: bfloat16 [4, 2048, 2560], P('dp', 'seq')
- step_grad: float32 [4, 40, 2048], P('dp', None, 'seq')
- weight_grad: float32 [2560, 1280], P('dp')
- filter_grads: float32 [5, 2816], replicated
- norm_grad: float32 [2560], replicated
- head_grads: float32 [3, 40], replicated
All inputs are finite; a program needn't handle non-finite values.
Results may differ from a plain program's by a relative error of at most 0.0029.
Values may be sent and summed in bfloat16 or wider, within the bound.
No kernel may reach another device: no remote copies, remote signals or barrier semaphores. Data moves between devices by JAX's collectives and lax.ppermute only.
A program may use at most 192 MiB of HBM per device.

v0:
```python
import jax
import jax.numpy as jnp
from jax import lax
from jax.sharding import PartitionSpec as P

HEADS = 40
HEAD_DIM = 64
STATE = 128
SPAN = 256
INNER = 2560
HIGHEST = lax.Precision.HIGHEST
MASKED = -1e30
EPSILON = 1e-05


def passed_along(value, axis, steps):
    count = lax.axis_size(axis)
    first, last = (max(0, -steps), min(count, count - steps))
    return lax.ppermute(value, axis, [(source, source + steps) for source in range(first, last)])


def entering_2(value, axis, combine, identity, reverse):
    length, position = (lax.axis_size(axis), lax.axis_index(axis))
    everything = jax.tree.map(lambda part: lax.all_gather(part, axis), value)
    start = jax.tree.map(
        lambda part, zero: jnp.broadcast_to(jnp.asarray(zero, part.dtype), part.shape),
        value,
        identity,
    )

    def lap(k, before):
        at = length - 1 - k if reverse else k
        reached = at > position if reverse else at < position
        new = combine(before, jax.tree.map(lambda part: part[at], everything))
        return jax.tree.map(lambda a, b: jnp.where(reached, a, b), new, before)

    return lax.fori_loop(0, length, lap, start)


def affine(earlier, later):
    return (earlier[0] * later[0], later[0][:, None, None] * earlier[1] + later[1])


def prepare(extended, step_rows, filter_taps, filter_bias, step_bias, decay_log):
    width = filter_taps.shape[0]
    length = extended.shape[0] - width + 1
    filtered = filter_bias + filter_taps[0] * extended[0:length]
    for offset in range(1, width):
        filtered = filtered + filter_taps[offset] * extended[offset : offset + length]
    activated = jax.nn.silu(filtered)
    step_sizes = jax.nn.softplus(step_rows + step_bias[:, None])
    decay_rates = step_sizes * (-jnp.exp(decay_log))[:, None]
    blocks = length // SPAN
    cumsums = jnp.cumsum(decay_rates.reshape(HEADS, blocks, SPAN), axis=2)
    values = activated[:, :INNER].reshape(blocks, SPAN, HEADS, HEAD_DIM)
    key_side = activated[:, INNER : INNER + STATE].reshape(blocks, SPAN, STATE)
    scaled = values * step_sizes.reshape(HEADS, blocks, SPAN).transpose(1, 2, 0)[..., None]
    to_end = jnp.exp(cumsums[:, :, -1:] - cumsums)
    block_states = jnp.einsum("hcs,cshp,csn->chpn", to_end, scaled, key_side, precision=HIGHEST)
    decays = jnp.exp(cumsums[:, :, -1]).T
    return (activated, cumsums, scaled, block_states, decays)


def summarize(block_states, decays):
    product = jnp.ones((decays.shape[1],), jnp.float32)
    running = jnp.zeros(block_states.shape[1:], jnp.float32)
    running = decays[0][:, None, None] * running + block_states[0]
    product = product * decays[0]
    return (product, running)


def finish(
    activated, cumsums, scaled, block_states, decays, entering, skip_gain, gate_rows, norm_weight
):
    blocks = cumsums.shape[1]
    length = blocks * SPAN
    values = activated[:, :INNER].reshape(blocks, SPAN, HEADS, HEAD_DIM)
    key_side = activated[:, INNER : INNER + STATE].reshape(blocks, SPAN, STATE)
    query_side = activated[:, INNER + STATE :].reshape(blocks, SPAN, STATE)
    starting = []
    starting.append(entering)
    starting = jnp.stack(starting)
    scores = jnp.einsum("ctn,csn->cts", query_side, key_side, precision=HIGHEST)
    differences = cumsums[:, :, :, None] - cumsums[:, :, None, :]
    causal = jnp.tril(jnp.ones((SPAN, SPAN), dtype=bool))
    weights = scores[None] * jnp.exp(jnp.where(causal, differences, MASKED))
    inside = jnp.einsum("hcts,cshp->cthp", weights, scaled, precision=HIGHEST)
    from_state = (
        jnp.einsum("ctn,chpn->cthp", query_side, starting, precision=HIGHEST)
        * jnp.exp(cumsums).transpose(1, 2, 0)[..., None]
    )
    result = inside + from_state + skip_gain[:, None] * values
    scanned = result.reshape(length, INNER)
    gated = scanned * jax.nn.silu(gate_rows)
    inverse_rms = lax.rsqrt(jnp.mean(gated * gated, axis=1, keepdims=True) + EPSILON)
    return gated * inverse_rms * norm_weight


def body(
    conv_input,
    gate_input,
    step_input,
    filter_taps,
    filter_bias,
    step_bias,
    decay_log,
    skip_gain,
    norm_weight,
    output_weight,
    output_grad,
):
    kernel_rows = filter_taps.shape[0] - 1
    raw_rows = conv_input[0]
    before = passed_along(raw_rows[-kernel_rows:], "seq", 1)
    extended = jnp.concatenate([before, raw_rows], axis=0).astype(jnp.float32)
    gate_rows = gate_input[0].astype(jnp.float32)
    step_rows = step_input[0]
    cotangent = output_grad[0]
    tokens = cotangent.shape[0]
    primals, pull_first = jax.vjp(
        prepare, extended, step_rows, filter_taps, filter_bias, step_bias, decay_log
    )
    activated, cumsums, scaled, block_states, decays = primals
    summary, pull_summary = jax.vjp(summarize, block_states, decays)
    identity = (jnp.ones_like(summary[0]), jnp.zeros_like(summary[1]))
    _, entering = entering_2(summary, "seq", affine, identity, False)
    normed, pull_second = jax.vjp(
        finish,
        activated,
        cumsums,
        scaled,
        block_states,
        decays,
        entering,
        skip_gain,
        gate_rows,
        norm_weight,
    )
    normed_low = normed.astype(jnp.bfloat16)
    groups = lax.axis_size("dp")
    own_rows = output_weight.shape[0]
    partial_columns = lax.dot_general(
        lax.all_gather(cotangent, "dp", axis=0, tiled=True),
        output_weight,
        (((1,), (1,)), ((), ())),
        preferred_element_type=jnp.float32,
    )
    regrouped = partial_columns.reshape(groups, tokens, own_rows)
    normed_grad = lax.all_to_all(regrouped, "dp", split_axis=0, concat_axis=2, tiled=True).reshape(
        tokens, groups * own_rows
    )
    weight_piece = lax.psum_scatter(
        lax.dot_general(
            normed_low, cotangent, (((0,), (0,)), ((), ())), preferred_element_type=jnp.float32
        ),
        "dp",
        scatter_dimension=0,
        tiled=True,
    )
    weight_grad = lax.psum(weight_piece, "seq")
    second = pull_second(normed_grad)
    (
        grad_activated,
        grad_cumsums,
        grad_scaled,
        grad_states,
        grad_decays,
        grad_entering,
        grad_skip,
        grad_gate,
        grad_norm,
    ) = second
    _, end_grad = entering_2((summary[0], grad_entering), "seq", affine, identity, True)
    decay_grad = jnp.sum(end_grad * entering, axis=(1, 2))
    more_states, more_decays = pull_summary((decay_grad, end_grad))
    first = pull_first(
        (
            grad_activated,
            grad_cumsums,
            grad_scaled,
            grad_states + more_states,
            grad_decays + more_decays,
        )
    )
    grad_extended, grad_steps, grad_taps, grad_bias, grad_step_bias, grad_decay_log = first
    returned = passed_along(grad_extended[:kernel_rows], "seq", -1)
    own_part = grad_extended[kernel_rows:]
    own_part = jnp.concatenate(
        [own_part[:-kernel_rows], own_part[-kernel_rows:] + returned], axis=0
    )
    filter_part = jnp.concatenate([grad_taps, grad_bias[None]], axis=0)
    head_part = jnp.stack([grad_step_bias, grad_decay_log, grad_skip])
    filter_grads, norm_grad, head_grads = lax.psum(
        (filter_part, grad_norm, head_part), ("seq", "dp")
    )
    input_grad = own_part.astype(jnp.bfloat16)[None]
    gate_grad = grad_gate.astype(jnp.bfloat16)[None]
    step_grad = grad_steps[None]
    return (input_grad, gate_grad, step_grad, weight_grad, filter_grads, norm_grad, head_grads)


def solution(mesh):
    return jax.shard_map(
        body,
        mesh=mesh,
        in_specs=(
            P("dp", "seq", None),
            P("dp", "seq", None),
            P("dp", None, "seq"),
            P(),
            P(),
            P(),
            P(),
            P(),
            P(),
            P("dp", None),
            P("dp", "seq", None),
        ),
        out_specs=(
            P("dp", "seq", None),
            P("dp", "seq", None),
            P("dp", None, "seq"),
            P("dp", None),
            P(),
            P(),
            P(),
        ),
        check_vma=False,
    )
```

profile of v0, /device:TPU:0, one launch (start us, length us, event | category | flops | bytes accessed | tf_op | source)
XLA Modules:
  0.0 764.4 jit_solution(17478603161339498694)
XLA Ops:
  8.8 4.9 collective-permute-start
  20.2 3.0 fusion.21
  24.7 1.9 slice.95
  26.6 3.2 copy.94
  29.8 5.0 fusion.69
  34.8 3.0 all-gather.8.cloned.1.call-done
  37.9 5.5 fusion.48
  43.4 4.7 all-to-all-start
  49.6 22.7 %all-reduce.15 = f32[320]{0:T(512)S(1)} all-reduce(f32[320]{0:T(512)S(1)} %dynamic-update-slice), channel_id=3, replica_groups=mesh['seq'=8,'dp'=4] {'seq'}, use_global_device_ids=true, to_apply=%add.15 | all-reduce | flops 320 | bytes 2560
  72.4 1.8 copy.100
  75.7 3.6 all-to-all-done
  79.4 3.2 copy.93
  82.6 108.8 %all-gather.10.cloned.1.call-done = f32[320,64,128]{2,1,0:T(8,128)} async-done(((f32[40,64,128]{2,1,0:T(8,128)}), f32[320,64,128]{2,1,0:T(8,128)}) %all-gather.10.cloned.1.call-update) | async-done | bytes 10485776 | tf_op jit(solution)/shard_map/all_gather | solution.py:24
  191.4 13.2 %while.30 = (s32[]{:T(128)}, f32[40,64,128]{2,1,0:T(8,128)S(1)}, s32[]{:T(128)}, f32[8,40]{1,0:T(8,128)S(1)}, f32[8,40,64,128]{3,2,1,0:T(8,128)}, /*index=5*/s32[]{:T(128)}, s32[]{:T(128)}) while((s32[]{:T(128)}, f32[40,64,128]{2,1,0:T(8,128)S(1)}, s32[]{:T(128)}, f32[8,40]{1,0:T(8,128)S(1)}, f32[8,40,64,128]{3,2,1,0:T(8,128)}, ...), condition=%wide.region_3.4_spmd.clone, body=%wide.region_2.3_spmd.clone.sunk | while | flops 1310724 | bytes 3932745 | solution.py:37
  204.6 3.3 fusion.93
  208.0 15.5 %multiply_reduce_fusion.8 = (f32[256]{0:T(256)S(1)}, f32[256]{0:T(256)S(1)}, f32[1,256,40,64]{1,3,2,0:T(8,128)S(1)}, f32[1,256,40,64]{1,3,2,0:T(8,128)}) fusion(f32[1,256,40,64]{1,3,2,0:T(8,128)} %bitcast.259, f32[40,64]{1,0:T(8,128)S(1)} %mul.591, f32[1,256,40,64]{1,3,2,0:T(8,128)} %bitcast.262, f32[1,256,40,64]{1,3,2,0:T(8,128)S(1)} %bitcast.254, ...), kind=kOutput, calls=%fused_computation.79 | convolution fusion | flops 2030960128 | bytes 18813088 | tf_op jit(solution)/shard_map/jvp(hcts,cshp->cthp)/dot_general | solution.py:87
  223.5 2.6 broadcast_multiply_fusion.5
  227.6 4.2 fusion.44
  231.8 8.5 %fusion.86 = f32[2560,1280]{1,0:T(8,128)} fusion(bf16[256,2560]{0,1:T(8,128)(2,1)S(1)} %bitcast.268, bf16[1,256,1280]{2,1,0:T(8,128)(2,1)} %param.25), kind=kOutput, calls=%fused_computation.114 | convolution fusion | flops 1677721600 | bytes 15073280 | tf_op jit(solution)/shard_map/dot_general | solution.py:153
  240.7 3.2 convert_element_type.75
  243.9 3.7 copy.129
  247.6 15.7 %fusion.8 = (f32[40,256]{1,0:T(8,128)S(1)}, f32[40,256]{1,0:T(8,128)}, f32[256,256]{1,0:T(8,128)S(1)}) fusion(f32[40,256]{1,0:T(8,128)S(1)} %get-tuple-element.347, f32[256,256]{1,0:T(8,128)S(1)} %copy-done.19, pred[256,256]{1,0:T(8,128)(4,1)S(1)} %iota_compare_fusion, f32[256,40,64]{0,2,1:T(8,128)S(1)} %bitcast.256, f32[256,40]{0,1:T(8,128)S(1)} %fusion.106, ...), kind=kOutput, calls=%fused_computation.13 | convolution fusion | flops 2037428224 | bytes 5996544 | tf_op jit(solution)/shard_map/transpose(jvp(hcts,cshp->cthp))/dot_general | solution.py:87
  263.3 3.2 copy.101
  266.5 3.2 copy.117
  269.7 4.3 fusion.33
  274.7 3.3 copy.106
  279.6 6.0 fusion.83
  286.9 3.2 fusion.29
  290.1 90.5 %all-gather.12.cloned.1.call-done = f32[320,64,128]{2,1,0:T(8,128)} async-done(((f32[40,64,128]{2,1,0:T(8,128)}), f32[320,64,128]{2,1,0:T(8,128)}) %all-gather.12.cloned.1.call-update) | async-done | bytes 10485776 | tf_op jit(solution)/shard_map/all_gather | solution.py:24
  380.6 21.0 %while.31 = (s32[]{:T(128)}, f32[40,64,128]{2,1,0:T(8,128)S(1)}, s32[]{:T(128)}, f32[8,40]{1,0:T(8,128)}, f32[8,40,64,128]{3,2,1,0:T(8,128)}, /*index=5*/s32[]{:T(128)}, s32[]{:T(128)}, s32[]{:T(128)}, s32[]{:T(128)}) while((s32[]{:T(128)}, f32[40,64,128]{2,1,0:T(8,128)S(1)}, s32[]{:T(128)}, f32[8,40]{1,0:T(8,128)}, ...), condition=%wide.region_8.9_spmd.clone, body=%wide.region_7.8_spmd.clone.sunk | while | flops 1310728 | bytes 3932807 | solution.py:37
  386.0 2.0 fusion.138
  391.1 2.1 fusion.138
  393.9 2.1 fusion.138
  396.7 2.1 fusion.138
  399.5 1.7 fusion.138
  402.2 5.5 fusion.39
  408.7 2.5 reduce-window.16
  411.5 12.6 %multiply_reduce_fusion.5 = (f32[40]{0:T(128)S(1)}, f32[256,40]{0,1:T(8,128)S(1)}, f32[1,256,40,64]{1,3,2,0:T(8,128)}) fusion(f32[1,256,40,64]{1,3,2,0:T(8,128)} %copy-done.9, f32[1,256,40,64]{1,3,2,0:T(8,128)} %bitcast.252, f32[256,40]{0,1:T(8,128)S(1)} %fusion.106, f32[256,40]{0,1:T(8,128)S(1)} %get-tuple-element.346, ...), kind=kOutput, calls=%fused_computation.75 | convolution fusion | flops 2025707520 | bytes 10977440 | tf_op jit(solution)/shard_map/transpose(jvp(hcts,cshp->cthp))/dot_general | solution.py:87
  424.1 3.4 copy.103
  427.5 6.1 fusion.80
  433.7 6.0 multiply_reduce_fusion.4
  441.5 4.4 fusion.26
  445.9 38.5 %reduce-scatter.2.cloned.1.call-done = f32[640,1280]{1,0:T(8,128)} async-done(((f32[2560,1280]{1,0:T(8,128)}), f32[640,1280]{1,0:T(8,128)}) %reduce-scatter.2.cloned.1.call-update) | async-done | bytes 3276816 | tf_op jit(solution)/shard_map/reduce_scatter | solution.py:152
  484.4 2.7 broadcast_multiply_fusion.3
  490.8 2.4 collective-permute-done.1
  494.4 120.0 %all-reduce.22.cloned.1.call-done = (f32[5,2816]{1,0:T(8,128)}, f32[2560]{0:T(1024)}, f32[3,40]{1,0:T(4,128)}) async-done(((f32[5,2816]{1,0:T(8,128)}, f32[2560]{0:T(1024)}, f32[3,40]{1,0:T(4,128)}), (f32[5,2816]{1,0:T(8,128)}, f32[2560]{0:T(1024)}, f32[3,40]{1,0:T(4,128)})) %all-reduce.22.cloned.1.call-update) | async-done | bytes 67056 | tf_op jit(solution)/shard_map/psum | solution.py:193
  614.4 137.1 %all-reduce.20.cloned.1.call-done = f32[640,1280]{1,0:T(8,128)} async-done(((f32[640,1280]{1,0:T(8,128)}), f32[640,1280]{1,0:T(8,128)}) %all-reduce.20.cloned.1.call-update) | async-done | bytes 3276816 | tf_op jit(solution)/shard_map/psum | solution.py:160
  751.5 4.0 copy.175
  (174 shorter events, 51.1 us)
Async XLA Ops:
  7.2 30.7 %copy-start = (bf16[640,1280]{1,0:T(8,128)(2,1)S(1)}, bf16[640,1280]{1,0:T(8,128)(2,1)}, u32[]{:S(2)}) copy-start(bf16[640,1280]{1,0:T(8,128)(2,1)} %param.24) | copy-start | bytes 4915204
  7.2 12.7 %copy-start.16 = (bf16[1,256,2816]{2,1,0:T(8,128)(2,1)S(1)}, bf16[1,256,2816]{2,1,0:T(8,128)(2,1)}, u32[]{:S(2)}) copy-start(bf16[1,256,2816]{2,1,0:T(8,128)(2,1)} %param.15) | copy-start | bytes 4325380
  7.2 30.7 %all-gather.8.cloned.1.call-start = ((), (), s32[]{:S(2)}) async-start(), calls=%async_computation.4 | async-start | bytes 3276800 | tf_op jit(solution)/shard_map/all_gather | solution.py:143
  7.9 183.4 %all-gather.10.cloned.1.call-start = ((), (), s32[]{:S(2)}) async-start(), calls=%async_computation.5 | async-start | bytes 11796480 | tf_op jit(solution)/shard_map/all_gather | solution.py:24
  8.8 11.1 %collective-permute-start = (bf16[3,2816]{1,0:T(4,128)(2,1)S(1)}, bf16[3,2816]{1,0:T(4,128)(2,1)S(1)}, u32[]{:S(2)}, u32[]{:S(2)}) collective-permute-start(bf16[3,2816]{1,0:T(4,128)(2,1)S(1)} %slice_bitcast_fusion), channel_id=1, source_target_pairs={{0,4},{4,8},{8,12},{12,16},{16,20},{20,24},{24,28},{1,5},{5,9},{9,... | collective-permute-start | bytes 50696 | tf_op jit(solution)/shard_map/ppermute | solution.py:19
  16.5 3.7 copy-start.24
  20.2 3.0 copy-start.2
  23.2 1.6 copy-start.12
  43.4 4.8 copy-start.31
  43.4 29.1 %copy-start.13 = (bf16[1,256,2560]{2,1,0:T(8,128)(2,1)S(1)}, bf16[1,256,2560]{2,1,0:T(8,128)(2,1)}, u32[]{:S(2)}) copy-start(bf16[1,256,2560]{2,1,0:T(8,128)(2,1)} %param.16) | copy-start | bytes 3932164
  43.4 36.0 %all-to-all-start = ((f32[4,256,640]{2,1,0:T(8,128)}), f32[4,256,640]{2,1,0:T(8,128)}, u32[]{:S(2)}, u32[]{:S(2)}) async-start(f32[4,256,640]{2,1,0:T(8,128)} %bitcast.271), calls=%async_computation | async-start | bytes 5242880 | tf_op jit(solution)/shard_map/all_to_all | solution.py:149
  48.0 26.2 %copy-start.22 = (f32[2560]{0:T(1024)S(1)}, f32[2560]{0:T(1024)}, u32[]{:S(2)}) copy-start(f32[2560]{0:T(1024)} %param.23) | copy-start | bytes 30724
  48.0 332.6 %all-gather.12.cloned.1.call-start = ((), (), s32[]{:S(2)}) async-start(), calls=%async_computation.6 | async-start | bytes 11796480 | tf_op jit(solution)/shard_map/all_gather | solution.py:24
  75.7 132.2 %copy-start.18 = (f32[256,256]{1,0:T(8,128)}, f32[256,256]{1,0:T(8,128)S(1)}, u32[]{:S(2)}) copy-start(f32[256,256]{1,0:T(8,128)S(1)} %fusion.98) | copy-start | bytes 786436
  204.6 18.9 %copy-start.27 = (f32[8,40]{1,0:T(8,128)}, f32[8,40]{1,0:T(8,128)S(1)}, u32[]{:S(2)}) copy-start(f32[8,40]{1,0:T(8,128)S(1)} %get-tuple-element.516) | copy-start | bytes 3844
  204.6 3.3 copy-start.4
  204.6 3.3 copy-start.29
  207.9 15.6 %copy-start.15 = (f32[256,40,64]{0,2,1:T(8,128)}, f32[256,40,64]{0,2,1:T(8,128)S(1)}, u32[]{:S(2)}) copy-start(f32[256,40,64]{0,2,1:T(8,128)S(1)} %fusion.93) | copy-start | bytes 7864324
  207.9 15.6 %copy-start.7 = (f32[1,256,4,640]{1,3,2,0:T(8,128)S(1)}, f32[1,256,4,640]{1,3,2,0:T(8,128)}, u32[]{:S(2)}) copy-start(f32[1,256,4,640]{1,3,2,0:T(8,128)} %copy.93) | copy-start | bytes 7864324
  208.0 15.6 %copy-start.11 = (f32[1,256,2560]{1,2,0:T(8,128)S(1)}, f32[1,256,2560]{1,2,0:T(8,128)}, u32[]{:S(2)}) copy-start(f32[1,256,2560]{1,2,0:T(8,128)} %copy.100) | copy-start | bytes 7864324
  226.1 1.5 copy-start.9
  231.8 252.6 %reduce-scatter.2.cloned.1.call-start = ((), (), s32[]{:S(2)}) async-start(), calls=%async_computation.2 | async-start | bytes 16384000 | tf_op jit(solution)/shard_map/reduce_scatter | solution.py:152
  240.4 374.0 %all-reduce.22.cloned.1.call-start = ((), (), s32[]{:S(2)}) async-start(), calls=%async_computation.7 | async-start | bytes 208896 | tf_op jit(solution)/shard_map/psum | solution.py:193
  240.7 7.0 copy-start.19
  243.9 3.8 copy-start.5
  243.9 3.8 copy-start.10
  277.9 8.9 %copy-start.6 = (f32[1,256,40,64]{1,3,2,0:T(8,128)S(1)}, f32[1,256,40,64]{1,3,2,0:T(8,128)}, u32[]{:S(2)}) copy-start(f32[1,256,40,64]{1,3,2,0:T(8,128)} %get-tuple-element.358) | copy-start | bytes 7864324
  277.9 8.9 %copy-start.8 = (f32[1,256,4,640]{1,3,2,0:T(8,128)S(1)}, f32[1,256,4,640]{1,3,2,0:T(8,128)}, u32[]{:S(2)}) copy-start(f32[1,256,4,640]{1,3,2,0:T(8,128)} %copy.93) | copy-start | bytes 7864324
  402.2 6.4 copy-start.23
  402.2 9.3 %copy-start.20 = (f32[256,256]{1,0:T(8,128)S(1)}, f32[256,256]{1,0:T(8,128)}, u32[]{:S(2)}) copy-start(f32[256,256]{1,0:T(8,128)} %copy-done.18) | copy-start | bytes 786436
  427.5 6.1 copy-start.3
  433.6 6.2 copy-start.17
  433.6 6.2 copy-start.26
  433.7 6.4 copy-start.30
  433.7 7.8 %copy-start.14 = (bf16[1,256,2560]{2,1,0:T(8,128)(2,1)S(1)}, bf16[1,256,2560]{2,1,0:T(8,128)(2,1)}, u32[]{:S(2)}) copy-start(bf16[1,256,2560]{2,1,0:T(8,128)(2,1)} %param.16) | copy-start | bytes 3932164
  441.4 310.1 %all-reduce.20.cloned.1.call-start = ((), (), s32[]{:S(2)}) async-start(), calls=%async_computation.3 | async-start | bytes 6553600 | tf_op jit(solution)/shard_map/psum | solution.py:160
  487.2 5.9 collective-permute-start.1
  751.5 5.8 copy-start.1
  751.5 4.0 copy-start.21
  751.5 4.6 copy-start.25
  751.5 5.2 copy-start.28
Sparse Core Ops, SparseCore 0:
  9.6 28.2 all-gather.7
  40.6 150.7 all-gather.9
  231.9 148.6 all-gather.11
  383.1 101.2 reduce-scatter.1
  490.8 123.6 all-reduce.21
  617.9 133.5 all-reduce.19
where the time goes:
time: 772 us; the launch traced here: 764 us
  waiting for transfers between devices  505 us (65%)
  matrix products  92.2 us (12%)
  other arithmetic  69.3 us (9%)
  local copies, waits for them, and re-layouts  47.8 us (6%)
  blocking collectives  22.7 us (3%)
  between operations  15.6 us (2%)
  starting transfers between devices  11.3 us (1%)
    all_gather x2, waiting for transfers between devices, entering_2(): everything = jax.tree.map(lambda part: lax.all_gather(part, axis), value)  199 us
    psum x1, waiting for transfers between devices, body(): weight_grad = lax.psum(weight_piece, 'seq')  137 us
    psum x1, waiting for transfers between devices, body(): lax.psum((filter_part, grad_norm, head_part), ('seq', 'dp'))  120 us
    dot_general x3, matrix products, finish(): inside = jnp.einsum('hcts,cshp->cthp', weights, scaled, precision=HIGHEST)  43.8 us
    reduce_scatter x1, waiting for transfers between devices, body(): lax.psum_scatter(lax.dot_general(normed_low, cotangent, (((0,), (0,)), ((...  38.5 us
    select_n x16, other arithmetic, lap(): return jax.tree.map(lambda a, b: jnp.where(reached, a, b), new, before)  27.8 us
    unnamed x1, blocking collectives  22.7 us
    dot_general x3, matrix products, prepare(): jnp.einsum('hcs,cshp,csn->chpn', to_end, scaled, key_side, precision=HIGH...  16.7 us
  transfers between devices with their start and end apart: 9, of which 8 were waited for; matrix products, arithmetic and copies ran while one was open for 21% of the time, Pallas kernels for 0%

commit v1 on v0

--- a/solution.py
+++ b/solution.py
@@ -157,7 +157,13 @@
         scatter_dimension=0,
         tiled=True,
     )
-    weight_grad = lax.psum(weight_piece, "seq")
+    devices = lax.axis_size("seq")
+    weight_grad, stride = (weight_piece, 1)
+    while stride < devices:
+        weight_grad = weight_grad + lax.ppermute(
+            weight_grad, "seq", [(i, i ^ stride) for i in range(devices)]
+        )
+        stride = 2 * stride
     second = pull_second(normed_grad)
     (
         grad_activated,

time: 772 us -> 893 us (1.16)
  waiting for transfers between devices: 505 us -> 611 us
  other arithmetic: 69.3 us -> 79.3 us
    ppermute x0 -> x3, waiting for transfers between devices: none -> 190 us  [body(): lax.ppermute(weight_grad, 'seq', [(i, i ^ stride) for i in range(devices)])]
    psum x1 -> x0, waiting for transfers between devices: 137 us -> none  [body(): weight_grad = lax.psum(weight_piece, 'seq')]
    all_gather x2, waiting for transfers between devices: 199 us -> 282 us  [entering_2(): everything = jax.tree.map(lambda part: lax.all_gather(part, axis), value)]
    psum x1, waiting for transfers between devices: 120 us -> 92.6 us  [body(): lax.psum((filter_part, grad_norm, head_part), ('seq', 'dp'))]
    add x0 -> x3, other arithmetic: none -> 14.4 us  [body(): weight_grad + lax.ppermute(weight_grad, 'seq', [(i, i ^ stride) for i in...]
  transfers between devices with their start and end apart: 9 -> 11, of which waited for: 8 -> 8; matrix products, arithmetic and copies ran while one was open for 21% -> 18% of each run, Pallas kernels for 0% -> 0%
where the time goes in v1:
time: 893 us; the launch traced here: 885 us
  waiting for transfers between devices  611 us (68%)
  matrix products  90.8 us (10%)
  other arithmetic  79.3 us (9%)
  local copies, waits for them, and re-layouts  50.7 us (6%)
  blocking collectives  22.7 us (3%)
  between operations  15.4 us (2%)
  starting transfers between devices  14.1 us (2%)
    all_gather x2, waiting for transfers between devices, entering_2(): everything = jax.tree.map(lambda part: lax.all_gather(part, axis), value)  282 us
    ppermute x3, waiting for transfers between devices, body(): lax.ppermute(weight_grad, 'seq', [(i, i ^ stride) for i in range(devices)])  190 us
    psum x1, waiting for transfers between devices, body(): lax.psum((filter_part, grad_norm, head_part), ('seq', 'dp'))  92.6 us
    dot_general x3, matrix products, finish(): inside = jnp.einsum('hcts,cshp->cthp', weights, scaled, precision=HIGHEST)  43.4 us
    reduce_scatter x1, waiting for transfers between devices, body(): lax.psum_scatter(lax.dot_general(normed_low, cotangent, (((0,), (0,)), ((...  39.4 us
    select_n x16, other arithmetic, lap(): return jax.tree.map(lambda a, b: jnp.where(reached, a, b), new, before)  25.8 us
    unnamed x1, blocking collectives  22.7 us
  transfers between devices with their start and end apart: 11, of which 8 were waited for; matrix products, arithmetic and copies ran while one was open for 18% of the time, Pallas kernels for 0%

profile of v1, /device:TPU:0, one launch (start us, length us, event | category | flops | bytes accessed | tf_op | source)
XLA Modules:
  0.0 885.2 jit_solution(12450058970826772173)
XLA Ops:
  8.8 4.9 collective-permute-start
  20.2 3.0 fusion.21
  24.7 1.9 slice.95
  26.6 3.2 copy.94
  29.8 5.0 fusion.69
  34.9 3.0 all-gather.8.cloned.1.call-done
  37.9 5.5 fusion.48
  43.4 4.7 all-to-all-start
  49.7 22.7 %all-reduce.15 = f32[320]{0:T(512)S(1)} all-reduce(f32[320]{0:T(512)S(1)} %dynamic-update-slice), channel_id=3, replica_groups=mesh['seq'=8,'dp'=4] {'seq'}, use_global_device_ids=true, to_apply=%add.15 | all-reduce | flops 320 | bytes 2560
  72.5 1.9 copy.100
  75.9 3.5 all-to-all-done
  79.4 3.2 copy.93
  82.7 108.5 %all-gather.10.cloned.1.call-done = f32[320,64,128]{2,1,0:T(8,128)} async-done(((f32[40,64,128]{2,1,0:T(8,128)}), f32[320,64,128]{2,1,0:T(8,128)}) %all-gather.10.cloned.1.call-update) | async-done | bytes 10485776 | tf_op jit(solution)/shard_map/all_gather | solution.py:24
  191.2 13.2 %while.30 = (s32[]{:T(128)}, f32[40,64,128]{2,1,0:T(8,128)S(1)}, s32[]{:T(128)}, f32[8,40]{1,0:T(8,128)S(1)}, f32[8,40,64,128]{3,2,1,0:T(8,128)}, /*index=5*/s32[]{:T(128)}, s32[]{:T(128)}) while((s32[]{:T(128)}, f32[40,64,128]{2,1,0:T(8,128)S(1)}, s32[]{:T(128)}, f32[8,40]{1,0:T(8,128)S(1)}, f32[8,40,64,128]{3,2,1,0:T(8,128)}, ...), condition=%wide.region_3.4_spmd.clone, body=%wide.region_2.3_spmd.clone.sunk | while | flops 1310724 | bytes 3932745 | solution.py:37
  192.8 1.6 fusion.137
  194.5 1.6 fusion.137
  204.4 3.3 fusion.93
  207.8 15.5 %multiply_reduce_fusion.8 = (f32[256]{0:T(256)S(1)}, f32[256]{0:T(256)S(1)}, f32[1,256,40,64]{1,3,2,0:T(8,128)S(1)}, f32[1,256,40,64]{1,3,2,0:T(8,128)}) fusion(f32[1,256,40,64]{1,3,2,0:T(8,128)} %bitcast.259, f32[40,64]{1,0:T(8,128)S(1)} %mul.591, f32[1,256,40,64]{1,3,2,0:T(8,128)} %bitcast.262, f32[1,256,40,64]{1,3,2,0:T(8,128)S(1)} %bitcast.254, ...), kind=kOutput, calls=%fused_computation.79 | convolution fusion | flops 2030960128 | bytes 18813088 | tf_op jit(solution)/shard_map/jvp(hcts,cshp->cthp)/dot_general | solution.py:87
  223.3 3.0 broadcast_multiply_fusion.5
  226.4 6.5 fusion.86
  233.0 5.0 fusion.44
  238.1 3.7 convert_element_type.75
  241.7 4.8 copy.129
  246.6 2.1 copy-done.12
  248.6 15.3 %fusion.8 = (f32[40,256]{1,0:T(8,128)S(1)}, f32[40,256]{1,0:T(8,128)}, f32[256,256]{1,0:T(8,128)S(1)}) fusion(f32[40,256]{1,0:T(8,128)S(1)} %get-tuple-element.347, f32[256,256]{1,0:T(8,128)S(1)} %fusion.98, pred[256,256]{1,0:T(8,128)(4,1)S(1)} %iota_compare_fusion, f32[256,40,64]{0,2,1:T(8,128)S(1)} %bitcast.256, f32[256,40]{0,1:T(8,128)S(1)} %fusion.106, ...), kind=kOutput, calls=%fused_computation.13 | convolution fusion | flops 2037428224 | bytes 5996544 | tf_op jit(solution)/shard_map/transpose(jvp(hcts,cshp->cthp))/dot_general | solution.py:87
  263.9 3.3 copy.101
  267.2 3.2 copy.117
  270.4 4.5 fusion.33
  275.5 3.2 copy.106
  278.7 1.6 fusion.101
  280.3 6.0 fusion.83
  287.7 3.4 fusion.29
  292.5 2.7 fusion.26
  295.2 39.4 %reduce-scatter.2.cloned.1.call-done = f32[640,1280]{1,0:T(8,128)} async-done(((f32[2560,1280]{1,0:T(8,128)}), f32[640,1280]{1,0:T(8,128)}) %reduce-scatter.2.cloned.1.call-update) | async-done | bytes 3276816 | tf_op jit(solution)/shard_map/reduce_scatter | solution.py:152
  336.0 173.8 %all-gather.12.cloned.1.call-done = f32[320,64,128]{2,1,0:T(8,128)} async-done(((f32[40,64,128]{2,1,0:T(8,128)}), f32[320,64,128]{2,1,0:T(8,128)}) %all-gather.12.cloned.1.call-update) | async-done | bytes 10485776 | tf_op jit(solution)/shard_map/all_gather | solution.py:24
  509.8 19.1 %while.31 = (s32[]{:T(128)}, f32[40,64,128]{2,1,0:T(8,128)S(1)}, s32[]{:T(128)}, f32[8,40]{1,0:T(8,128)}, f32[8,40,64,128]{3,2,1,0:T(8,128)}, /*index=5*/s32[]{:T(128)}, s32[]{:T(128)}, s32[]{:T(128)}, s32[]{:T(128)}) while((s32[]{:T(128)}, f32[40,64,128]{2,1,0:T(8,128)S(1)}, s32[]{:T(128)}, f32[8,40]{1,0:T(8,128)}, ...), condition=%wide.region_8.9_spmd.clone, body=%wide.region_7.8_spmd.clone.sunk | while | flops 1310728 | bytes 3932807 | solution.py:37
  529.4 5.6 fusion.39
  536.0 2.5 reduce-window.16
  538.7 12.6 %multiply_reduce_fusion.5 = (f32[40]{0:T(128)S(1)}, f32[256,40]{0,1:T(8,128)S(1)}, f32[1,256,40,64]{1,3,2,0:T(8,128)}) fusion(f32[1,256,40,64]{1,3,2,0:T(8,128)} %get-tuple-element.342, f32[1,256,40,64]{1,3,2,0:T(8,128)} %bitcast.252, f32[256,40]{0,1:T(8,128)S(1)} %fusion.106, f32[256,40]{0,1:T(8,128)S(1)} %get-tuple-element.346, ...), kind=kOutput, calls=%fused_computation.75 | convolution fusion | flops 2025707520 | bytes 10977440 | tf_op jit(solution)/shard_map/transpose(jvp(hcts,cshp->cthp))/dot_general | solution.py:87
  551.4 4.3 add.287
  555.8 3.4 copy.103
  559.6 6.2 fusion.80
  565.8 4.9 multiply_reduce_fusion.4
  571.7 56.6 %collective-permute-done.3 = f32[640,1280]{1,0:T(8,128)} collective-permute-done((f32[640,1280]{1,0:T(8,128)}, f32[640,1280]{1,0:T(8,128)}, u32[]{:S(2)}, u32[]{:S(2)}) %collective-permute-start.3) | collective-permute-done | bytes 3276832 | tf_op jit(solution)/shard_map/ppermute | solution.py:163
  628.2 5.0 add.288
  643.6 133.2 %collective-permute-done.4 = f32[640,1280]{1,0:T(8,128)} collective-permute-done((f32[640,1280]{1,0:T(8,128)}, f32[640,1280]{1,0:T(8,128)}, u32[]{:S(2)}, u32[]{:S(2)}) %collective-permute-start.4) | collective-permute-done | bytes 3276832 | tf_op jit(solution)/shard_map/ppermute | solution.py:163
  776.8 5.0 add.289
  781.8 92.6 %all-reduce.19.cloned.1.call-done = (f32[5,2816]{1,0:T(8,128)}, f32[2560]{0:T(1024)}, f32[3,40]{1,0:T(4,128)}) async-done(((f32[5,2816]{1,0:T(8,128)}, f32[2560]{0:T(1024)}, f32[3,40]{1,0:T(4,128)}), (f32[5,2816]{1,0:T(8,128)}, f32[2560]{0:T(1024)}, f32[3,40]{1,0:T(4,128)})) %all-reduce.19.cloned.1.call-update) | async-done | bytes 67056 | tf_op jit(solution)/shard_map/psum | solution.py:199
  (207 shorter events, 62.7 us)
Async XLA Ops:
  7.2 30.7 %copy-start = (bf16[640,1280]{1,0:T(8,128)(2,1)S(1)}, bf16[640,1280]{1,0:T(8,128)(2,1)}, u32[]{:S(2)}) copy-start(bf16[640,1280]{1,0:T(8,128)(2,1)} %param.24) | copy-start | bytes 4915204
  7.2 12.7 %copy-start.23 = (bf16[1,256,2816]{2,1,0:T(8,128)(2,1)S(1)}, bf16[1,256,2816]{2,1,0:T(8,128)(2,1)}, u32[]{:S(2)}) copy-start(bf16[1,256,2816]{2,1,0:T(8,128)(2,1)} %param.15) | copy-start | bytes 4325380
  7.2 30.7 %all-gather.8.cloned.1.call-start = ((), (), s32[]{:S(2)}) async-start(), calls=%async_computation.3 | async-start | bytes 3276800 | tf_op jit(solution)/shard_map/all_gather | solution.py:143
  7.9 183.3 %all-gather.10.cloned.1.call-start = ((), (), s32[]{:S(2)}) async-start(), calls=%async_computation.4 | async-start | bytes 11796480 | tf_op jit(solution)/shard_map/all_gather | solution.py:24
  8.8 11.1 %collective-permute-start = (bf16[3,2816]{1,0:T(4,128)(2,1)S(1)}, bf16[3,2816]{1,0:T(4,128)(2,1)S(1)}, u32[]{:S(2)}, u32[]{:S(2)}) collective-permute-start(bf16[3,2816]{1,0:T(4,128)(2,1)S(1)} %slice_bitcast_fusion), channel_id=1, source_target_pairs={{0,4},{4,8},{8,12},{12,16},{16,20},{20,24},{24,28},{1,5},{5,9},{9,... | collective-permute-start | bytes 50696 | tf_op jit(solution)/shard_map/ppermute | solution.py:19
  16.5 3.7 copy-start.36
  17.8 5.4 copy-start.38
  18.8 227.7 %copy-start.31 = (f32[40,256]{1,0:T(8,128)}, f32[40,256]{1,0:T(8,128)S(1)}, u32[]{:S(2)}) copy-start(f32[40,256]{1,0:T(8,128)S(1)} %get-tuple-element.347) | copy-start | bytes 122884
  43.4 4.8 copy-start.45
  43.4 29.1 %copy-start.15 = (bf16[1,256,2560]{2,1,0:T(8,128)(2,1)S(1)}, bf16[1,256,2560]{2,1,0:T(8,128)(2,1)}, u32[]{:S(2)}) copy-start(bf16[1,256,2560]{2,1,0:T(8,128)(2,1)} %param.16) | copy-start | bytes 3932164
  43.4 36.1 %all-to-all-start = ((f32[4,256,640]{2,1,0:T(8,128)}), f32[4,256,640]{2,1,0:T(8,128)}, u32[]{:S(2)}, u32[]{:S(2)}) async-start(f32[4,256,640]{2,1,0:T(8,128)} %bitcast.271), calls=%async_computation | async-start | bytes 5242880 | tf_op jit(solution)/shard_map/all_to_all | solution.py:149
  48.1 26.3 %copy-start.29 = (f32[2560]{0:T(1024)S(1)}, f32[2560]{0:T(1024)}, u32[]{:S(2)}) copy-start(f32[2560]{0:T(1024)} %param.23) | copy-start | bytes 30724
  48.1 286.5 %reduce-scatter.2.cloned.1.call-start = ((), (), s32[]{:S(2)}) async-start(), calls=%async_computation.2 | async-start | bytes 16384000 | tf_op jit(solution)/shard_map/reduce_scatter | solution.py:152
  74.5 172.0 %copy-start.27 = (pred[256,256]{1,0:T(8,128)(4,1)}, pred[256,256]{1,0:T(8,128)(4,1)S(1)}, u32[]{:S(2)}) copy-start(pred[256,256]{1,0:T(8,128)(4,1)S(1)} %iota_compare_fusion) | copy-start | bytes 196612
  75.9 170.6 %copy-start.25 = (f32[256,256]{1,0:T(8,128)}, f32[256,256]{1,0:T(8,128)S(1)}, u32[]{:S(2)}) copy-start(f32[256,256]{1,0:T(8,128)S(1)} %fusion.98) | copy-start | bytes 786436
  204.4 18.8 %copy-start.42 = (f32[8,40]{1,0:T(8,128)}, f32[8,40]{1,0:T(8,128)S(1)}, u32[]{:S(2)}) copy-start(f32[8,40]{1,0:T(8,128)S(1)} %get-tuple-element.513) | copy-start | bytes 3844
  207.7 15.5 %copy-start.19 = (f32[256,40,64]{0,2,1:T(8,128)}, f32[256,40,64]{0,2,1:T(8,128)S(1)}, u32[]{:S(2)}) copy-start(f32[256,40,64]{0,2,1:T(8,128)S(1)} %fusion.93) | copy-start | bytes 7864324
  207.7 15.5 %copy-start.10 = (f32[1,256,4,640]{1,3,2,0:T(8,128)S(1)}, f32[1,256,4,640]{1,3,2,0:T(8,128)}, u32[]{:S(2)}) copy-start(f32[1,256,4,640]{1,3,2,0:T(8,128)} %copy.93) | copy-start | bytes 7864324
  207.8 15.5 %copy-start.13 = (f32[1,256,2560]{1,2,0:T(8,128)S(1)}, f32[1,256,2560]{1,2,0:T(8,128)}, u32[]{:S(2)}) copy-start(f32[1,256,2560]{1,2,0:T(8,128)} %copy.100) | copy-start | bytes 7864324
  232.9 276.9 %all-gather.12.cloned.1.call-start = ((), (), s32[]{:S(2)}) async-start(), calls=%async_computation.5 | async-start | bytes 11796480 | tf_op jit(solution)/shard_map/all_gather | solution.py:24
  238.0 636.4 %all-reduce.19.cloned.1.call-start = ((), (), s32[]{:S(2)}) async-start(), calls=%async_computation.6 | async-start | bytes 208896 | tf_op jit(solution)/shard_map/psum | solution.py:199
  241.7 4.8 copy-start.8
  241.7 6.9 copy-start.12
  278.7 8.9 %copy-start.9 = (f32[1,256,40,64]{1,3,2,0:T(8,128)S(1)}, f32[1,256,40,64]{1,3,2,0:T(8,128)}, u32[]{:S(2)}) copy-start(f32[1,256,40,64]{1,3,2,0:T(8,128)} %get-tuple-element.358) | copy-start | bytes 7864324
  278.7 8.9 %copy-start.11 = (f32[1,256,4,640]{1,3,2,0:T(8,128)S(1)}, f32[1,256,4,640]{1,3,2,0:T(8,128)}, u32[]{:S(2)}) copy-start(f32[1,256,4,640]{1,3,2,0:T(8,128)} %copy.93) | copy-start | bytes 7864324
  278.7 8.9 %copy-start.35 = (f32[256]{0:T(256)S(1)}, f32[256]{0:T(256)}, u32[]{:S(2)}) copy-start(f32[256]{0:T(256)} %copy-done.34) | copy-start | bytes 3076
  287.6 3.9 copy-start.17
  287.6 4.9 copy-start.18
  287.6 4.9 copy-start.30
  334.6 216.8 %collective-permute-start.2 = (f32[640,1280]{1,0:T(8,128)}, f32[640,1280]{1,0:T(8,128)}, u32[]{:S(2)}, u32[]{:S(2)}) collective-permute-start(f32[640,1280]{1,0:T(8,128)} %reduce-scatter.2.cloned.1.call-done), channel_id=1, source_target_pairs={{0,4},{4,0},{8,12},{12,8},{16,20},{20,16},{24,28},{28,24},{1,5},{5... | collective-permute-start | bytes 9830408 | tf_op jit(solution)/shard_map/ppermute | solution.py:163
  529.4 5.6 copy-start.39
  529.4 6.5 copy-start.33
  529.4 9.3 %copy-start.26 = (f32[256,256]{1,0:T(8,128)S(1)}, f32[256,256]{1,0:T(8,128)}, u32[]{:S(2)}) copy-start(f32[256,256]{1,0:T(8,128)} %copy-done.25) | copy-start | bytes 786436
  529.4 9.3 %copy-start.28 = (pred[256,256]{1,0:T(8,128)(4,1)S(1)}, pred[256,256]{1,0:T(8,128)(4,1)}, u32[]{:S(2)}) copy-start(pred[256,256]{1,0:T(8,128)(4,1)} %copy-done.27) | copy-start | bytes 196612
  529.4 9.3 %copy-start.32 = (f32[40,256]{1,0:T(8,128)S(1)}, f32[40,256]{1,0:T(8,128)}, u32[]{:S(2)}) copy-start(f32[40,256]{1,0:T(8,128)} %copy-done.31) | copy-start | bytes 122884
  538.7 12.6 %copy-start.21 = (f32[640,1280]{1,0:T(8,128)S(1)}, f32[640,1280]{1,0:T(8,128)}, u32[]{:S(2)}) copy-start(f32[640,1280]{1,0:T(8,128)} %reduce-scatter.2.cloned.1.call-done) | copy-start | bytes 9830404
  555.7 72.6 %collective-permute-start.3 = (f32[640,1280]{1,0:T(8,128)}, f32[640,1280]{1,0:T(8,128)}, u32[]{:S(2)}, u32[]{:S(2)}) collective-permute-start(f32[640,1280]{1,0:T(8,128)} %add.287), channel_id=1, source_target_pairs={{0,8},{4,12},{8,0},{12,4},{16,24},{20,28},{24,16},{28,20},{1,9},{5... | collective-permute-start | bytes 9830408 | tf_op jit(solution)/shard_map/ppermute | solution.py:163
  555.8 3.6 copy-start.24
  555.8 3.6 copy-start.37
  555.8 3.6 copy-start.41
  559.2 6.6 copy-start.3
  571.6 65.7 %copy-start.4 = (f32[256,2816]{1,0:T(8,128)}, f32[256,2816]{1,0:T(8,128)S(1)}, u32[]{:S(2)}) copy-start(f32[256,2816]{1,0:T(8,128)S(1)} %get-tuple-element.351) | copy-start | bytes 8650756
  571.6 65.7 %copy-start.5 = (f32[256,2816]{1,0:T(8,128)}, f32[256,2816]{1,0:T(8,128)S(1)}, u32[]{:S(2)}) copy-start(f32[256,2816]{1,0:T(8,128)S(1)} %get-tuple-element.352) | copy-start | bytes 8650756
  571.6 65.7 %copy-start.6 = (f32[256,2816]{1,0:T(8,128)}, f32[256,2816]{1,0:T(8,128)S(1)}, u32[]{:S(2)}) copy-start(f32[256,2816]{1,0:T(8,128)S(1)} %get-tuple-element.353) | copy-start | bytes 8650756
  571.6 63.1 %copy-start.44 = (f32[40]{0:T(128)S(1)}, f32[40]{0:T(128)}, u32[]{:S(2)}) copy-start(f32[40]{0:T(128)} %param.21) | copy-start | bytes 484
  633.3 143.5 %collective-permute-start.4 = (f32[640,1280]{1,0:T(8,128)}, f32[640,1280]{1,0:T(8,128)}, u32[]{:S(2)}, u32[]{:S(2)}) collective-permute-start(f32[640,1280]{1,0:T(8,128)} %add.288), channel_id=1, source_target_pairs={{0,16},{4,20},{8,24},{12,28},{16,0},{20,4},{24,8},{28,12},{1,17},{... | collective-permute-start | bytes 9830408 | tf_op jit(solution)/shard_map/ppermute | solution.py:163
  634.9 6.0 collective-permute-start.1
  642.4 236.1 %copy-start.1 = (bf16[640,1280]{1,0:T(8,128)(2,1)S(1)}, bf16[640,1280]{1,0:T(8,128)(2,1)}, u32[]{:S(2)}) copy-start(bf16[640,1280]{1,0:T(8,128)(2,1)} %param.24) | copy-start | bytes 4915204
  (9 other events, 23.9 us)
Sparse Core Ops, SparseCore 0:
  9.6 28.2 all-gather.7
  40.6 150.5 all-gather.9
  233.0 101.4 reduce-scatter.1
  337.2 172.5 all-gather.11
  641.0 233.2 all-reduce.18
